TPU v7x, 256 devices: a whole 4x4x8 slice. The times are simulated.
256 devices in a mesh: lat: 16 (over x, y), lon: 16 (over z, core).
Axes of the slice: x: 4, y: 4, z: 8, core: 2. Of those that a mesh axis runs over, the one named last changes fastest.
Arguments:
- transport: bfloat16 [48, 2048, 6144], P(None, 'lat', 'lon'), may hold values from -0.046875 to 0.046875
- sigma_class: int32 [48, 2048, 6144], P(None, 'lat', 'lon'), may hold values from 0 to 199
- basin_id: int32 [2048, 6144], P('lat', 'lon'), may hold values from 0 to 3
- depth_levels: int32 [2048, 6144], P('lat', 'lon'), may hold values from 0 to 48
Outputs:
- overturning: bfloat16 [4, 200, 2048], replicated
Inputs may be any that keep to these rules, and one draw needn't show every extreme that they name: `depth_levels`: 0 marks a land column.
All inputs are finite; a program needn't handle non-finite values.
Results may differ from a plain program's by a relative error of at most 0.001.
Values may be sent and summed in bfloat16 or wider, within the bound.
A program may use at most 64 MiB of HBM per device.

v0:
```python
import jax
import jax.numpy as jnp
from jax import lax
from jax.sharding import PartitionSpec as P

CLASSES = 200
BASINS = 4


def over_pieces(array, axis):
    return lax.all_gather(array, axis).sum(0)


def bin_rows(transport, sigma_class, basin_id, depth_levels):
    depth_count, row_count, col_count = sigma_class.shape
    block_rows = 8
    block_count = row_count // block_rows
    cell_count = depth_count * col_count
    level_index = lax.broadcasted_iota(jnp.int32, (block_rows, depth_count, col_count), 1)
    class_iota = lax.broadcasted_iota(jnp.int32, (1, CLASSES, 1), 1)
    basin_iota = lax.broadcasted_iota(jnp.int32, (1, BASINS, 1), 1)

    def one_block(start):
        flow = jnp.transpose(lax.dynamic_slice_in_dim(transport, start, block_rows, 1), (1, 0, 2))
        klass = jnp.transpose(
            lax.dynamic_slice_in_dim(sigma_class, start, block_rows, 1), (1, 0, 2)
        )
        basin = lax.dynamic_slice_in_dim(basin_id, start, block_rows, 0)
        depth = lax.dynamic_slice_in_dim(depth_levels, start, block_rows, 0)
        wet_cells = level_index < depth[:, None, :]
        masked = jnp.where(wet_cells, flow, jnp.zeros_like(flow)).reshape(block_rows, 1, cell_count)
        basin_cells = jnp.broadcast_to(
            basin[:, None, :], (block_rows, depth_count, col_count)
        ).reshape(block_rows, 1, cell_count)
        basin_flow = jnp.where(basin_cells == basin_iota, masked, jnp.zeros_like(masked))
        class_hot = (klass.reshape(block_rows, 1, cell_count) == class_iota).astype(jnp.bfloat16)
        return jnp.einsum("rcn,rbn->rbc", class_hot, basin_flow, preferred_element_type=jnp.float32)

    starts = jnp.arange(block_count) * block_rows
    tables = lax.map(one_block, starts)
    return jnp.transpose(tables.reshape(row_count, BASINS, CLASSES), (1, 2, 0))


def body(transport, sigma_class, basin_id, depth_levels):
    table = bin_rows(transport, sigma_class, basin_id, depth_levels)
    summed = over_pieces(table, "lon")
    overturn = jnp.cumsum(summed, axis=1).astype(jnp.bfloat16)
    return lax.all_gather(overturn, "lat", axis=2, tiled=True)


def solution(mesh):
    placed = (P(None, "lat", "lon"), P(None, "lat", "lon"), P("lat", "lon"), P("lat", "lon"))
    return jax.shard_map(body, mesh=mesh, in_specs=placed, out_specs=P(), check_vma=False)
```

profile of v0, /device:TPU:1, one launch (start us, length us, event | category | flops | bytes accessed | tf_op | source)
XLA Modules:
  0.0 510.2 jit_solution(1347658050803611538)
XLA Ops:
  6.5 381.1 %while.11 = (s32[]{:T(128)}, f32[16,8,4,200]{3,1,0,2:T(8,128)S(1)}, s32[16]{0:T(128)S(1)}, s32[128,384]{1,0:T(8,128)}, s32[128,384]{1,0:T(8,128)}, /*index=5*/bf...) while((s32[]{:T(128)}, f32[16,8,4,200]{3,1,0,2:T(8,128)S(1)}, ...), condition=%wide.region_1.2_spmd.clone, body=%wide.region_0.1_spmd.clone.sunk | while | flops 266895360 | bytes 3998891 | solution.py:40
  9.3 0.8 constant_dynamic-slice_fusion.6
  10.1 1.2 fusion.24
  11.3 1.4 constant_dynamic-slice_fusion.5
  12.7 17.7 %fusion.25 = f32[1,8,4,200]{3,2,1,0:T(4,128)S(1)} fusion(s32[8,18432]{1,0:T(8,128)S(1)} %bitcast.34, s32[8,18432]{1,0:T(8,128)S(1)} %bitcast.33, bf16[8,18432]{1,0:T(8,128)(2,1)S(1)} %bitcast.35), kind=kOutput, calls=%fused_computation.9.clone.1 | convolution fusion | flops 266600448 | bytes 1500160 | tf_op jit(solution)/shard_map/while/body/eval_jaxpr/rcn,rbn->rbc/dot_general | solution.py:37
  33.1 0.8 constant_dynamic-slice_fusion.6
  33.9 1.2 fusion.24
  35.1 1.4 constant_dynamic-slice_fusion.5
  36.5 17.7 %fusion.25 = f32[1,8,4,200]{3,2,1,0:T(4,128)S(1)} fusion(s32[8,18432]{1,0:T(8,128)S(1)} %bitcast.34, s32[8,18432]{1,0:T(8,128)S(1)} %bitcast.33, bf16[8,18432]{1,0:T(8,128)(2,1)S(1)} %bitcast.35), kind=kOutput, calls=%fused_computation.9.clone.1 | convolution fusion | flops 266600448 | bytes 1500160 | tf_op jit(solution)/shard_map/while/body/eval_jaxpr/rcn,rbn->rbc/dot_general | solution.py:37
  57.0 0.8 constant_dynamic-slice_fusion.6
  57.7 1.2 fusion.24
  59.0 1.4 constant_dynamic-slice_fusion.5
  60.3 17.7 %fusion.25 = f32[1,8,4,200]{3,2,1,0:T(4,128)S(1)} fusion(s32[8,18432]{1,0:T(8,128)S(1)} %bitcast.34, s32[8,18432]{1,0:T(8,128)S(1)} %bitcast.33, bf16[8,18432]{1,0:T(8,128)(2,1)S(1)} %bitcast.35), kind=kOutput, calls=%fused_computation.9.clone.1 | convolution fusion | flops 266600448 | bytes 1500160 | tf_op jit(solution)/shard_map/while/body/eval_jaxpr/rcn,rbn->rbc/dot_general | solution.py:37
  80.8 0.8 constant_dynamic-slice_fusion.6
  81.6 1.2 fusion.24
  82.8 1.4 constant_dynamic-slice_fusion.5
  84.2 17.7 %fusion.25 = f32[1,8,4,200]{3,2,1,0:T(4,128)S(1)} fusion(s32[8,18432]{1,0:T(8,128)S(1)} %bitcast.34, s32[8,18432]{1,0:T(8,128)S(1)} %bitcast.33, bf16[8,18432]{1,0:T(8,128)(2,1)S(1)} %bitcast.35), kind=kOutput, calls=%fused_computation.9.clone.1 | convolution fusion | flops 266600448 | bytes 1500160 | tf_op jit(solution)/shard_map/while/body/eval_jaxpr/rcn,rbn->rbc/dot_general | solution.py:37
  104.7 0.8 constant_dynamic-slice_fusion.6
  105.4 1.2 fusion.24
  106.7 1.4 constant_dynamic-slice_fusion.5
  108.0 17.7 %fusion.25 = f32[1,8,4,200]{3,2,1,0:T(4,128)S(1)} fusion(s32[8,18432]{1,0:T(8,128)S(1)} %bitcast.34, s32[8,18432]{1,0:T(8,128)S(1)} %bitcast.33, bf16[8,18432]{1,0:T(8,128)(2,1)S(1)} %bitcast.35), kind=kOutput, calls=%fused_computation.9.clone.1 | convolution fusion | flops 266600448 | bytes 1500160 | tf_op jit(solution)/shard_map/while/body/eval_jaxpr/rcn,rbn->rbc/dot_general | solution.py:37
  128.5 0.8 constant_dynamic-slice_fusion.6
  129.3 1.2 fusion.24
  130.5 1.4 constant_dynamic-slice_fusion.5
  131.9 17.7 %fusion.25 = f32[1,8,4,200]{3,2,1,0:T(4,128)S(1)} fusion(s32[8,18432]{1,0:T(8,128)S(1)} %bitcast.34, s32[8,18432]{1,0:T(8,128)S(1)} %bitcast.33, bf16[8,18432]{1,0:T(8,128)(2,1)S(1)} %bitcast.35), kind=kOutput, calls=%fused_computation.9.clone.1 | convolution fusion | flops 266600448 | bytes 1500160 | tf_op jit(solution)/shard_map/while/body/eval_jaxpr/rcn,rbn->rbc/dot_general | solution.py:37
  152.3 0.8 constant_dynamic-slice_fusion.6
  153.1 1.2 fusion.24
  154.4 1.4 constant_dynamic-slice_fusion.5
  155.7 17.7 %fusion.25 = f32[1,8,4,200]{3,2,1,0:T(4,128)S(1)} fusion(s32[8,18432]{1,0:T(8,128)S(1)} %bitcast.34, s32[8,18432]{1,0:T(8,128)S(1)} %bitcast.33, bf16[8,18432]{1,0:T(8,128)(2,1)S(1)} %bitcast.35), kind=kOutput, calls=%fused_computation.9.clone.1 | convolution fusion | flops 266600448 | bytes 1500160 | tf_op jit(solution)/shard_map/while/body/eval_jaxpr/rcn,rbn->rbc/dot_general | solution.py:37
  176.2 0.8 constant_dynamic-slice_fusion.6
  176.9 1.2 fusion.24
  178.2 1.4 constant_dynamic-slice_fusion.5
  179.6 17.7 %fusion.25 = f32[1,8,4,200]{3,2,1,0:T(4,128)S(1)} fusion(s32[8,18432]{1,0:T(8,128)S(1)} %bitcast.34, s32[8,18432]{1,0:T(8,128)S(1)} %bitcast.33, bf16[8,18432]{1,0:T(8,128)(2,1)S(1)} %bitcast.35), kind=kOutput, calls=%fused_computation.9.clone.1 | convolution fusion | flops 266600448 | bytes 1500160 | tf_op jit(solution)/shard_map/while/body/eval_jaxpr/rcn,rbn->rbc/dot_general | solution.py:37
  200.0 0.8 constant_dynamic-slice_fusion.6
  200.8 1.2 fusion.24
  202.0 1.4 constant_dynamic-slice_fusion.5
  203.4 17.7 %fusion.25 = f32[1,8,4,200]{3,2,1,0:T(4,128)S(1)} fusion(s32[8,18432]{1,0:T(8,128)S(1)} %bitcast.34, s32[8,18432]{1,0:T(8,128)S(1)} %bitcast.33, bf16[8,18432]{1,0:T(8,128)(2,1)S(1)} %bitcast.35), kind=kOutput, calls=%fused_computation.9.clone.1 | convolution fusion | flops 266600448 | bytes 1500160 | tf_op jit(solution)/shard_map/while/body/eval_jaxpr/rcn,rbn->rbc/dot_general | solution.py:37
  223.9 0.8 constant_dynamic-slice_fusion.6
  224.6 1.2 fusion.24
  225.9 1.4 constant_dynamic-slice_fusion.5
  227.2 17.7 %fusion.25 = f32[1,8,4,200]{3,2,1,0:T(4,128)S(1)} fusion(s32[8,18432]{1,0:T(8,128)S(1)} %bitcast.34, s32[8,18432]{1,0:T(8,128)S(1)} %bitcast.33, bf16[8,18432]{1,0:T(8,128)(2,1)S(1)} %bitcast.35), kind=kOutput, calls=%fused_computation.9.clone.1 | convolution fusion | flops 266600448 | bytes 1500160 | tf_op jit(solution)/shard_map/while/body/eval_jaxpr/rcn,rbn->rbc/dot_general | solution.py:37
  248.5 1.2 fusion.24
  249.7 1.4 constant_dynamic-slice_fusion.5
  251.1 17.7 %fusion.25 = f32[1,8,4,200]{3,2,1,0:T(4,128)S(1)} fusion(s32[8,18432]{1,0:T(8,128)S(1)} %bitcast.34, s32[8,18432]{1,0:T(8,128)S(1)} %bitcast.33, bf16[8,18432]{1,0:T(8,128)(2,1)S(1)} %bitcast.35), kind=kOutput, calls=%fused_computation.9.clone.1 | convolution fusion | flops 266600448 | bytes 1500160 | tf_op jit(solution)/shard_map/while/body/eval_jaxpr/rcn,rbn->rbc/dot_general | solution.py:37
  272.3 1.2 fusion.24
  273.6 1.4 constant_dynamic-slice_fusion.5
  274.9 17.7 %fusion.25 = f32[1,8,4,200]{3,2,1,0:T(4,128)S(1)} fusion(s32[8,18432]{1,0:T(8,128)S(1)} %bitcast.34, s32[8,18432]{1,0:T(8,128)S(1)} %bitcast.33, bf16[8,18432]{1,0:T(8,128)(2,1)S(1)} %bitcast.35), kind=kOutput, calls=%fused_computation.9.clone.1 | convolution fusion | flops 266600448 | bytes 1500160 | tf_op jit(solution)/shard_map/while/body/eval_jaxpr/rcn,rbn->rbc/dot_general | solution.py:37
  296.2 1.2 fusion.24
  297.4 1.4 constant_dynamic-slice_fusion.5
  298.8 17.7 %fusion.25 = f32[1,8,4,200]{3,2,1,0:T(4,128)S(1)} fusion(s32[8,18432]{1,0:T(8,128)S(1)} %bitcast.34, s32[8,18432]{1,0:T(8,128)S(1)} %bitcast.33, bf16[8,18432]{1,0:T(8,128)(2,1)S(1)} %bitcast.35), kind=kOutput, calls=%fused_computation.9.clone.1 | convolution fusion | flops 266600448 | bytes 1500160 | tf_op jit(solution)/shard_map/while/body/eval_jaxpr/rcn,rbn->rbc/dot_general | solution.py:37
  320.0 1.2 fusion.24
  321.3 1.4 constant_dynamic-slice_fusion.5
  322.6 17.7 %fusion.25 = f32[1,8,4,200]{3,2,1,0:T(4,128)S(1)} fusion(s32[8,18432]{1,0:T(8,128)S(1)} %bitcast.34, s32[8,18432]{1,0:T(8,128)S(1)} %bitcast.33, bf16[8,18432]{1,0:T(8,128)(2,1)S(1)} %bitcast.35), kind=kOutput, calls=%fused_computation.9.clone.1 | convolution fusion | flops 266600448 | bytes 1500160 | tf_op jit(solution)/shard_map/while/body/eval_jaxpr/rcn,rbn->rbc/dot_general | solution.py:37
  343.8 1.2 fusion.24
  345.1 1.4 constant_dynamic-slice_fusion.5
  346.4 17.7 %fusion.25 = f32[1,8,4,200]{3,2,1,0:T(4,128)S(1)} fusion(s32[8,18432]{1,0:T(8,128)S(1)} %bitcast.34, s32[8,18432]{1,0:T(8,128)S(1)} %bitcast.33, bf16[8,18432]{1,0:T(8,128)(2,1)S(1)} %bitcast.35), kind=kOutput, calls=%fused_computation.9.clone.1 | convolution fusion | flops 266600448 | bytes 1500160 | tf_op jit(solution)/shard_map/while/body/eval_jaxpr/rcn,rbn->rbc/dot_general | solution.py:37
  367.7 1.1 fusion.24
  368.8 1.1 constant_dynamic-slice_fusion.5
  369.9 17.7 %fusion.25 = f32[1,8,4,200]{3,2,1,0:T(4,128)S(1)} fusion(s32[8,18432]{1,0:T(8,128)S(1)} %bitcast.34, s32[8,18432]{1,0:T(8,128)S(1)} %bitcast.33, bf16[8,18432]{1,0:T(8,128)(2,1)S(1)} %bitcast.35), kind=kOutput, calls=%fused_computation.9.clone.1 | convolution fusion | flops 266600448 | bytes 1500160 | tf_op jit(solution)/shard_map/while/body/eval_jaxpr/rcn,rbn->rbc/dot_general | solution.py:37
  387.7 1.0 copy.13
  388.7 51.5 %all-gather.6.cloned.1.call-done = f32[64,200,128]{2,1,0:T(8,128)} async-done(((f32[4,200,128]{2,1,0:T(8,128)}), f32[64,200,128]{2,1,0:T(8,128)}) %all-gather.6.cloned.1.call-update) | async-done | bytes 6553616 | tf_op jit(solution)/shard_map/all_gather | solution.py:11
  440.2 3.2 reduce_sum.9
  444.9 54.4 %all-gather.4.cloned.1.call-done = bf16[4,200,2048]{2,1,0:T(8,128)(2,1)} async-done(((bf16[4,200,128]{2,1,0:T(8,128)(2,1)}), bf16[4,200,2048]{2,1,0:T(8,128)(2,1)}) %all-gather.4.cloned.1.call-update) | async-done | bytes 3276816 | tf_op jit(solution)/shard_map/all_gather | solution.py:48
  499.3 4.1 copy.35
  (68 shorter events, 17.6 us)
Async XLA Ops:
  6.5 433.7 %all-gather.6.cloned.1.call-start = ((), (), s32[]{:S(2)}) async-start(), calls=%async_computation.1 | async-start | bytes 6963200 | tf_op jit(solution)/shard_map/all_gather | solution.py:11
  388.6 110.7 %all-gather.4.cloned.1.call-start = ((), (), s32[]{:S(2)}) async-start(), calls=%async_computation | async-start | bytes 3481600 | tf_op jit(solution)/shard_map/all_gather | solution.py:48
Sparse Core Ops, SparseCore 0:
  388.8 51.3 all-gather.5
  445.0 54.2 all-gather.3
where the time goes:
time: 513 us; the launch traced here: 510 us
  matrix products  283 us (55%)
  waiting for transfers between devices  106 us (21%)
  local copies, waits for them, and re-layouts  51 us (10%)
  loops' own time  33.8 us (7%)
  other arithmetic  23 us (4%)
  between operations  13.4 us (3%)
    dot_general x16, matrix products, one_block(): jnp.einsum('rcn,rbn->rbc', class_hot, basin_flow, preferred_element_type=...  283 us
    all_gather x1, waiting for transfers between devices, body(): return lax.all_gather(overturn, 'lat', axis=2, tiled=True)  54.4 us
    all_gather x1, waiting for transfers between devices, over_pieces(): return lax.all_gather(array, axis).sum(0)  51.5 us
    another operation x1, loops' own time, bin_rows(): tables = lax.map(one_block, starts)  33.8 us
    dynamic_slice x16, local copies, waits for them, and re-layouts, one_block(): lax.dynamic_slice_in_dim(sigma_class, start, block_rows, 1)  21.4 us
    select_n x16, other arithmetic, one_block(): jnp.where(wet_cells, flow, jnp.zeros_like(flow))  19.1 us
    dynamic_slice x16, local copies, waits for them, and re-layouts, one_block(): depth = lax.dynamic_slice_in_dim(depth_levels, start, block_rows, 0)  12.3 us
    dynamic_slice x16, local copies, waits for them, and re-layouts, bin_rows(): tables = lax.map(one_block, starts)  10.7 us
  transfers between devices with their start and end apart: 2, of which 2 were waited for; matrix products, arithmetic and copies ran while one was open for 0% of the time, Pallas kernels for 0%

commit v1 on v0

v1 whole, which is shorter than its diff:
```python
import functools

import jax
import jax.numpy as jnp
from jax import lax
from jax.experimental import pallas as pl
from jax.experimental.pallas import tpu as pltpu
from jax.sharding import PartitionSpec as P

CLASSES = 200
BASINS = 4
LOW = 32
HIGH = 7
SUB = 8
PER_STEP = 4
LANES = 128


def one_hot_kernel(flow_ref, class_ref, basin_ref, depth_ref, out_ref):
    levels, rows, cols = class_ref.shape
    tiles = cols // LANES
    m = BASINS * HIGH * SUB
    n = LOW * SUB

    def twice(x):
        return jnp.concatenate([x, x - 1.0], axis=0).astype(jnp.bfloat16)

    def run(*accs):
        def step(s, _):
            for sub in range(rows // SUB):
                r = pl.ds(sub * SUB, SUB)
                pieces = []
                for level in range(PER_STEP):
                    k = s * PER_STEP + level
                    for tile in range(tiles):
                        pieces.append((k, pl.ds(tile * LANES, LANES)))
                halves = []
                for index, (k, c) in enumerate(pieces):
                    klass = class_ref[k, r, c]
                    high = basin_ref[r, c] * HIGH + (klass >> 5)
                    wet = k < depth_ref[r, c]
                    high = jnp.where(wet, high, -100)
                    low = klass & (LOW - 1)
                    flow = flow_ref[k, r, c].astype(jnp.float32)
                    halves.append((
                        twice(high.astype(jnp.float32)),
                        twice(low.astype(jnp.float32)),
                        jnp.concatenate([flow, flow], axis=0).astype(jnp.bfloat16),
                    ))
                    if len(halves) < 2:
                        continue
                    high2, low2, flow2 = [jnp.concatenate(h, axis=1) for h in zip(*halves)]
                    halves = []
                    zero = jnp.zeros_like(flow2)
                    one = jnp.ones_like(flow2)
                    rhs = jnp.concatenate(
                        [jnp.where(low2 == jnp.bfloat16(2 * u), one, zero) for u in range(LOW // 2)], axis=0
                    )
                    lhs = jnp.concatenate(
                        [jnp.where(high2 == jnp.bfloat16(2 * t), flow2, zero) for t in range(BASINS * HIGH // 2)], axis=0
                    )
                    q = (index // 2) % 2
                    reg = (index // 4) % 2
                    pltpu.matmul_push_rhs(rhs, staging_register=reg, mxu_index=q, transpose=True)
                    pltpu.matmul_acc_lhs(accs[2 * sub + q], lhs, load_staged_rhs=reg)
            return 0

        lax.fori_loop(0, levels // PER_STEP, step, 0)
        row = lax.broadcasted_iota(jnp.int32, (1, SUB, n), 1)
        col = lax.broadcasted_iota(jnp.int32, (1, SUB, n), 2)
        own = (col % SUB) == row
        for sub in range(rows // SUB):
            both = pltpu.matmul_pop(accs[2 * sub]) + pltpu.matmul_pop(accs[2 * sub + 1])
            cube = both.reshape(m // SUB, SUB, n)
            out_ref[sub] = jnp.sum(jnp.where(own, cube, 0.0), axis=1)

    accs = [pltpu.ACC(q)((m, n), jnp.float32) for _ in range(rows // SUB) for q in range(2)]
    pl.run_scoped(run, *accs)


def bin_rows(transport, sigma_class, basin_id, depth_levels):
    levels, rows, cols = sigma_class.shape
    step_rows = 2 * SUB
    groups = rows // SUB
    return pl.pallas_call(
        one_hot_kernel,
        grid=(rows // step_rows,),
        in_specs=[
            pl.BlockSpec((levels, step_rows, cols), lambda g: (0, g, 0)),
            pl.BlockSpec((levels, step_rows, cols), lambda g: (0, g, 0)),
            pl.BlockSpec((step_rows, cols), lambda g: (g, 0)),
            pl.BlockSpec((step_rows, cols), lambda g: (g, 0)),
        ],
        out_specs=pl.BlockSpec((2, BASINS * HIGH, LOW * SUB), lambda g: (g, 0, 0)),
        out_shape=jax.ShapeDtypeStruct((groups, BASINS * HIGH, LOW * SUB), jnp.float32),
        compiler_params=pltpu.CompilerParams(dimension_semantics=("arbitrary",)),
    )(transport, sigma_class, basin_id, depth_levels)


def body(transport, sigma_class, basin_id, depth_levels):
    table = bin_rows(transport, sigma_class, basin_id, depth_levels)
    table = lax.psum_scatter(table, "lon", scatter_dimension=0, tiled=True)[0]
    table = table.reshape(BASINS, HIGH * LOW, SUB)[:, :CLASSES]
    overturn = jnp.cumsum(table, axis=1).astype(jnp.bfloat16)
    return lax.all_gather(overturn, ("lat", "lon"), axis=2, tiled=True)


def solution(mesh):
    placed = (P(None, "lat", "lon"), P(None, "lat", "lon"), P("lat", "lon"), P("lat", "lon"))

    def run(*args):
        return jax.shard_map(body, mesh=mesh, in_specs=placed, out_specs=P(), check_vma=False)(*args)

    return run
```

time: 513 us -> 247 us (0.48)
  matrix products: 283 us -> 0 us
  waiting for transfers between devices: 106 us -> 169 us
  Pallas kernels: 0 us -> 53.6 us
  local copies, waits for them, and re-layouts: 51 us -> 7.39 us
  loops' own time: 33.8 us -> 0 us
  other arithmetic: 23 us -> 2.97 us
    dot_general x16 -> x0, matrix products: 283 us -> none  [one_block(): jnp.einsum('rcn,rbn->rbc', class_hot, basin_flow, preferred_element_type=...]
    reduce_scatter x0 -> x1, waiting for transfers between devices: none -> 58.5 us  [body(): table = lax.psum_scatter(table, 'lon', scatter_dimension=0, tiled=True)[0]]
    pallas_call x0 -> x1, Pallas kernels: none -> 53.6 us  [bin_rows(): pl.pallas_call(one_hot_kernel, grid=(rows // step_rows,), in_specs=[pl.Bl...]
    dynamic_slice x48 -> x0, local copies, waits for them, and re-layouts: 44.4 us -> none  [the longest x16 21.4 us: one_block(): lax.dynamic_slice_in_dim(sigma_class, start, block_rows, 1)]
    another operation x1 -> x0, loops' own time: 33.8 us -> none  [bin_rows(): tables = lax.map(one_block, starts)]
    select_n x16 -> x0, other arithmetic: 19.1 us -> none  [one_block(): jnp.where(wet_cells, flow, jnp.zeros_like(flow))]
    all_gather x0 -> x1, local copies, waits for them, and re-layouts: none -> 5.98 us  [body(): return lax.all_gather(overturn, ('lat', 'lon'), axis=2, tiled=True)]
    all_gather x2 -> x1, waiting for transfers between devices: 106 us -> 110 us  [body(): return lax.all_gather(overturn, ('lat', 'lon'), axis=2, tiled=True)]
where the time goes in v1:
time: 247 us; the launch traced here: 246 us
  waiting for transfers between devices  169 us (68%)
  Pallas kernels  53.6 us (22%)
  between operations  13.4 us (5%)
  local copies, waits for them, and re-layouts  7.39 us (3%)
  other arithmetic  2.97 us (1%)
    all_gather x1, waiting for transfers between devices, body(): return lax.all_gather(overturn, ('lat', 'lon'), axis=2, tiled=True)  110 us
    reduce_scatter x1, waiting for transfers between devices, body(): table = lax.psum_scatter(table, 'lon', scatter_dimension=0, tiled=True)[0]  58.5 us
    pallas_call x1, Pallas kernels, bin_rows(): pl.pallas_call(one_hot_kernel, grid=(rows // step_rows,), in_specs=[pl.Bl...  53.6 us
    all_gather x1, local copies, waits for them, and re-layouts, body(): return lax.all_gather(overturn, ('lat', 'lon'), axis=2, tiled=True)  5.98 us
  transfers between devices with their start and end apart: 2, of which 2 were waited for; matrix products, arithmetic and copies ran while one was open for 0% of the time, Pallas kernels for 0%

profile of v1, /device:TPU:1, one launch (start us, length us, event | category | flops | bytes accessed | tf_op | source)
XLA Modules:
  0.0 246.3 jit_solution(18057486400425885939)
XLA Ops:
  6.5 0.0 reduce-scatter.2.cloned.1.call-start
  6.5 53.6 %shard_map.46 = f32[16,28,256]{2,1,0:T(8,128)} custom-call(bf16[48,128,384]{2,1,0:T(8,128)(2,1)} %flow_ref.1, s32[48,128,384]{2,1,0:T(8,128)} %class_ref.1, s32[128,384]{1,0:T(8,128)} %basin_ref.1, s32[128,384]{1,0:T(8,128)} %depth_ref.1), custom_call_target="tpu_custom_call" | custom-call | tf_op jit(solution)/shard_map/pallas_call | solution.py:85
  60.2 0.0 reduce-scatter.2.cloned.1.call-update
  60.2 0.0 all-gather.2.cloned.1.call-start
  60.2 58.5 %reduce-scatter.2.cloned.1.call-done = f32[1,28,256]{2,1,0:T(8,128)} async-done(((f32[16,28,256]{2,1,0:T(8,128)}), f32[1,28,256]{2,1,0:T(8,128)}) %reduce-scatter.2.cloned.1.call-update) | async-done | bytes 28688 | tf_op jit(solution)/shard_map/reduce_scatter | solution.py:102
  118.7 1.0 reshape_squeeze.3
  119.8 0.2 copy.11
  120.0 2.3 reduce-window.6
  122.2 0.1 slice.15
  122.3 0.1 copy.8
  122.5 0.7 fusion
  123.1 0.0 all-gather.2.cloned.1.call-update
  123.2 110.3 %all-gather.2.cloned.1.call-done = bf16[4,200,2048]{1,2,0:T(8,128)(2,1)} async-done(((bf16[4,200,8]{1,2,0:T(8,128)(2,1)}), bf16[4,200,2048]{1,2,0:T(8,128)(2,1)}) %all-gather.2.cloned.1.call-update) | async-done | bytes 3276816 | tf_op jit(solution)/shard_map/all_gather | solution.py:105
  233.4 6.0 %copy.10 = bf16[4,200,2048]{2,1,0:T(8,128)(2,1)} copy(bf16[4,200,2048]{1,2,0:T(8,128)(2,1)} %all-gather.2.cloned.1.call-done) | data formatting | bytes 6553600 | tf_op jit(solution)/shard_map/all_gather | solution.py:105
  (5 shorter events, 0.1 us)
Async XLA Ops:
  6.5 112.2 %reduce-scatter.2.cloned.1.call-start = ((), (), s32[]{:S(2)}) async-start(), calls=%async_computation.1 | async-start | bytes 557056 | tf_op jit(solution)/shard_map/reduce_scatter | solution.py:102
  60.2 173.3 %all-gather.2.cloned.1.call-start = ((), (), s32[]{:S(2)}) async-start(), calls=%async_computation.2 | async-start | bytes 4210688 | tf_op jit(solution)/shard_map/all_gather | solution.py:105
Sparse Core Ops, SparseCore 0:
  60.3 58.4 reduce-scatter.1
  123.3 110.0 all-gather.1

commit v2 on v1

--- a/solution.py
+++ b/solution.py
@@ -54,7 +54,7 @@
                     zero = jnp.zeros_like(flow2)
                     one = jnp.ones_like(flow2)
                     rhs = jnp.concatenate(
-                        [jnp.where(low2 == jnp.bfloat16(2 * u), one, zero) for u in range(LOW // 2)], axis=0
+                        [jnp.where(low2 <= jnp.bfloat16(2 * u), one, zero) for u in range(LOW // 2)], axis=0
                     )
                     lhs = jnp.concatenate(
                         [jnp.where(high2 == jnp.bfloat16(2 * t), flow2, zero) for t in range(BASINS * HIGH // 2)], axis=0
@@ -69,10 +69,24 @@
         row = lax.broadcasted_iota(jnp.int32, (1, SUB, n), 1)
         col = lax.broadcasted_iota(jnp.int32, (1, SUB, n), 2)
         own = (col % SUB) == row
+        lane = lax.broadcasted_iota(jnp.int32, (BASINS * HIGH, LANES), 1)
         for sub in range(rows // SUB):
+            group = pl.program_id(0) * (rows // SUB) + sub
             both = pltpu.matmul_pop(accs[2 * sub]) + pltpu.matmul_pop(accs[2 * sub + 1])
             cube = both.reshape(m // SUB, SUB, n)
-            out_ref[sub] = jnp.sum(jnp.where(own, cube, 0.0), axis=1)
+            part = jnp.sum(jnp.where(own, cube, 0.0), axis=1)
+            whole = jnp.where(lane >= LANES - SUB, part[:, n - LANES :], 0.0)
+            for shift in (SUB, 2 * SUB, 4 * SUB, 8 * SUB):
+                whole = whole + pltpu.roll(whole, shift, 1)
+            for basin in range(BASINS):
+                before = jnp.zeros((1, LANES), jnp.float32)
+                for digit in range(HIGH):
+                    h = basin * HIGH + digit
+                    for half in range(n // LANES):
+                        out_ref[h, half, pl.ds(group, 1), :] = (
+                            part[h : h + 1, half * LANES : (half + 1) * LANES] + before
+                        )
+                    before = before + whole[h : h + 1]
 
     accs = [pltpu.ACC(q)((m, n), jnp.float32) for _ in range(rows // SUB) for q in range(2)]
     pl.run_scoped(run, *accs)
@@ -82,6 +96,7 @@
     levels, rows, cols = sigma_class.shape
     step_rows = 2 * SUB
     groups = rows // SUB
+    shape = (BASINS * HIGH, LOW * SUB // LANES, groups, LANES)
     return pl.pallas_call(
         one_hot_kernel,
         grid=(rows // step_rows,),
@@ -91,24 +106,185 @@
             pl.BlockSpec((step_rows, cols), lambda g: (g, 0)),
             pl.BlockSpec((step_rows, cols), lambda g: (g, 0)),
         ],
-        out_specs=pl.BlockSpec((2, BASINS * HIGH, LOW * SUB), lambda g: (g, 0, 0)),
-        out_shape=jax.ShapeDtypeStruct((groups, BASINS * HIGH, LOW * SUB), jnp.float32),
+        out_specs=pl.BlockSpec(shape, lambda g: (0, 0, 0, 0)),
+        out_shape=jax.ShapeDtypeStruct(shape, jnp.float32),
         compiler_params=pltpu.CompilerParams(dimension_semantics=("arbitrary",)),
     )(transport, sigma_class, basin_id, depth_levels)
 
 
-def body(transport, sigma_class, basin_id, depth_levels):
+def spread_kernel(
+    n_lat, n_lon, side, table_ref, out_ref, parts, shuffle,
+    sum_send, sum_recv, z_send, z_recv, one_send, one_recv, two_send, two_recv, pair_send, pair_recv,
+):
+    owners, size, _ = table_ref.shape
+    chunks = owners // 2
+    lat, lon = lax.axis_index("lat"), lax.axis_index("lon")
+    x, y = lat // side, lax.rem(lat, side)
+    z, core = lon // 2, lax.rem(lon, 2)
+    depth = n_lon // 2
+
+    def at(to_lat, to_lon):
+        return {"lat": to_lat, "lon": to_lon}
+
+    def along(axis, d):
+        if axis == 0:
+            return lax.rem(x + d, side) * side + y
+        return x * side + lax.rem(y + d, side)
+
+    def block(chunk, of_lat):
+        rows = pl.ds(pl.multiple_of((2 * chunk + core) * size, size), size)
+        return out_ref.at[rows, pl.ds(pl.multiple_of(of_lat * LANES, LANES), LANES)]
+
+    def send(src, dst, send_sem, recv_sem, to):
+        copy = pltpu.make_async_remote_copy(
+            src_ref=src, dst_ref=dst, send_sem=send_sem, recv_sem=recv_sem,
+            device_id=to, device_id_type=pl.DeviceIdType.MESH,
+        )
+        return copy
+
+    barrier = pltpu.get_barrier_semaphore()
+    for d in range(1, n_lon):
+        pl.semaphore_signal(barrier, inc=1, device_id=at(lat, lax.rem(lon + d, n_lon)), device_id_type=pl.DeviceIdType.MESH)
+    for axis in range(2):
+        for d in range(1, side):
+            pl.semaphore_signal(barrier, inc=1, device_id=at(along(axis, d), lon), device_id_type=pl.DeviceIdType.MESH)
+    pl.semaphore_wait(barrier, n_lon - 1 + 2 * (side - 1))
+
+    def share(d):
+        to = lax.rem(lon + d, n_lon)
+        return to, send(table_ref.at[lax.rem(to, owners)], parts.at[d - 1], sum_send.at[d - 1], sum_recv.at[d - 1], at(lat, to))
+
+    for d in range(1, n_lon):
+        to, copy = share(d)
+
+        @pl.when(to < owners)
+        def _():
+            copy.start()
+
+    groups = LANES // SUB
+    line = lax.broadcasted_iota(jnp.int32, (LANES, LANES), 0)
+    lane = lax.broadcasted_iota(jnp.int32, (LANES, LANES), 1) % SUB
+    for low in range(groups):
+        shuffle[:, low * LANES : (low + 1) * LANES] = jnp.where(line == lane + low * SUB, 1.0, 0.0).astype(jnp.bfloat16)
+
+    partner = at(lat, z * 2 + 1 - core)
+
+    def to_pair(chunk, of_lat):
+        send(block(chunk, of_lat), block(chunk, of_lat), pair_send, pair_recv, partner).start()
+
+    @pl.when(lon < owners)
+    def _():
+        total = table_ref[lax.rem(lon, owners)]
+        for d in range(1, n_lon):
+            share(d)[1].wait_recv()
+            total = total + parts[d - 1]
+        wide = jnp.dot(total.astype(jnp.bfloat16), shuffle[...], preferred_element_type=jnp.float32)
+        row = lax.broadcasted_iota(jnp.int32, (size // groups, groups, LANES), 1)
+        col = lax.broadcasted_iota(jnp.int32, (size // groups, groups, LANES), 2)
+        own = row == col // SUB
+        lines = []
+        for low in range(groups):
+            piece = wide[:, low * LANES : (low + 1) * LANES].reshape(size // groups, groups, LANES)
+            lines.append(jnp.sum(jnp.where(own, piece, 0.0), axis=1, keepdims=True))
+        mine = jnp.concatenate(lines, axis=1).reshape(size, LANES)
+        block(z, lat)[...] = mine.astype(jnp.bfloat16)
+        for d in range(1, depth):
+            to = lax.rem(z + d, depth) * 2 + core
+            send(block(z, lat), block(z, lat), z_send.at[d - 1], z_recv.at[z], at(lat, to)).start()
+
+    def first(chunk, d):
+        return send(block(chunk, lat), block(chunk, lat), one_send.at[chunk, d - 1], one_recv.at[chunk, d - 1],
+                    at(along(chunk % 2, d), lon))
+
+    def second(chunk, of, of_lat, d):
+        return send(block(chunk, of_lat), block(chunk, of_lat), two_send, two_recv.at[chunk, of, d - 1],
+                    at(along(1 - chunk % 2, d), lon))
+
+    def came(chunk, d):
+        return along(chunk % 2, side - d)
+
+    def came_twice(chunk, of, d):
+        if chunk % 2 == 0:
+            return lax.rem(x + (side - of), side) * side + lax.rem(y + (side - d), side)
+        return lax.rem(x + (side - d), side) * side + lax.rem(y + (side - of), side)
+
+    for chunk in range(chunks):
+
+        @pl.when(z != chunk)
+        def _():
+            send(block(chunk, lat), block(chunk, lat), z_send.at[0], z_recv.at[chunk], at(lat, lon)).wait_recv()
+
+        for d in range(1, side):
+            first(chunk, d).start()
+        for d in range(1, side):
+            second(chunk, 0, lat, d).start()
+        to_pair(chunk, lat)
+    for chunk in range(chunks):
+        for of in range(1, side):
+            first(chunk, of).wait_recv()
+            for d in range(1, side):
+                second(chunk, of, came(chunk, of), d).start()
+            to_pair(chunk, came(chunk, of))
+    for chunk in range(chunks):
+        for of in range(side):
+            for d in range(1, side):
+                second(chunk, of, lat, d).wait_recv()
+                to_pair(chunk, came_twice(chunk, of, d))
+
+    for d in range(1, n_lon):
+        to, copy = share(d)
+
+        @pl.when(to < owners)
+        def _():
+            copy.wait_send()
+
+    @pl.when(lon < owners)
+    def _():
+        for d in range(1, depth):
+            send(block(z, lat), block(z, lat), z_send.at[d - 1], z_recv.at[z], at(lat, lon)).wait_send()
+
+    for chunk in range(chunks):
+        for d in range(1, side):
+            first(chunk, d).wait_send()
+    seconds = out_ref.at[pl.ds(0, chunks * side * (side - 1) * size // n_lat)]
+    pltpu.make_async_copy(seconds, seconds, two_send).wait()
+    half = out_ref.at[pl.ds(0, chunks * size)]
+    pltpu.make_async_copy(half, half, pair_send).wait()
+    pltpu.make_async_copy(half, half, pair_recv).wait()
+
+
+def spread(table, n_lat, n_lon):
+    owners, size, _ = table.shape
+    side = 4
+    chunks = owners // 2
+    dma = pltpu.SemaphoreType.DMA
+    return pl.pallas_call(
+        functools.partial(spread_kernel, n_lat, n_lon, side),
+        out_shape=jax.ShapeDtypeStruct((owners * size, n_lat * LANES), jnp.bfloat16),
+        in_specs=[pl.BlockSpec(memory_space=pltpu.VMEM)],
+        out_specs=pl.BlockSpec(memory_space=pltpu.VMEM),
+        scratch_shapes=[
+            pltpu.VMEM((n_lon - 1, size, LANES), jnp.float32),
+            pltpu.VMEM((LANES, LANES // SUB * LANES), jnp.bfloat16),
+            dma((n_lon - 1,)), dma((n_lon - 1,)),
+            dma((n_lon // 2 - 1,)), dma((chunks,)),
+            dma((chunks, side - 1)), dma((chunks, side - 1)),
+            dma, dma((chunks, side, side - 1)),
+            dma, dma,
+        ],
+        compiler_params=pltpu.CompilerParams(collective_id=0, has_side_effects=True),
+    )(table)
+
+
+def body(n_lat, n_lon, transport, sigma_class, basin_id, depth_levels):
     table = bin_rows(transport, sigma_class, basin_id, depth_levels)
-    table = lax.psum_scatter(table, "lon", scatter_dimension=0, tiled=True)[0]
-    table = table.reshape(BASINS, HIGH * LOW, SUB)[:, :CLASSES]
-    overturn = jnp.cumsum(table, axis=1).astype(jnp.bfloat16)
-    return lax.all_gather(overturn, ("lat", "lon"), axis=2, tiled=True)
+    groups = table.shape[2]
+    table = table.reshape(BASINS * HIGH * 2 // 4, 4 * groups, LANES)
+    overturn = spread(table, n_lat, n_lon)
+    return overturn.reshape(BASINS, HIGH * LOW, -1)[:, :CLASSES]
 
 
 def solution(mesh):
     placed = (P(None, "lat", "lon"), P(None, "lat", "lon"), P("lat", "lon"), P("lat", "lon"))
-
-    def run(*args):
-        return jax.shard_map(body, mesh=mesh, in_specs=placed, out_specs=P(), check_vma=False)(*args)
-
-    return run
+    run = functools.partial(body, mesh.shape["lat"], mesh.shape["lon"])
+    return jax.shard_map(run, mesh=mesh, in_specs=placed, out_specs=P(), check_vma=False)

time: 247 us -> 108 us (0.44)
  waiting for transfers between devices: 169 us -> 0 us
  Pallas kernels: 53.6 us -> 104 us
  between operations: 13.4 us -> 0.01 us
  local copies, waits for them, and re-layouts: 7.39 us -> 4.07 us
  other arithmetic: 2.97 us -> 0 us
    all_gather x1 -> x0, waiting for transfers between devices: 110 us -> none  [body(): return lax.all_gather(overturn, ('lat', 'lon'), axis=2, tiled=True)]
    reduce_scatter x1 -> x0, waiting for transfers between devices: 58.5 us -> none  [body(): table = lax.psum_scatter(table, 'lon', scatter_dimension=0, tiled=True)[0]]
    pallas_call x0 -> x1, Pallas kernels: none -> 47.9 us  [spread(): pl.pallas_call(functools.partial(spread_kernel, n_lat, n_lon, side), out_...]
    all_gather x1 -> x0, local copies, waits for them, and re-layouts: 5.98 us -> none  [body(): return lax.all_gather(overturn, ('lat', 'lon'), axis=2, tiled=True)]
    slice x2 -> x1, local copies, waits for them, and re-layouts: 0.19 us -> 4.07 us  [body(): return overturn.reshape(BASINS, HIGH * LOW, -1)[:, :CLASSES]]
    another operation x3 -> x0, other arithmetic: 2.97 us -> none  [run(): jax.shard_map(body, mesh=mesh, in_specs=placed, out_specs=P(), check_vma=...]
  transfers between devices with their start and end apart: 2 -> 0, of which waited for: 2 -> 0; matrix products, arithmetic and copies ran while one was open for 0% -> 0% of each run, Pallas kernels for 0% -> 0%
where the time goes in v2:
time: 108 us
  Pallas kernels  104 us (96%)
  local copies, waits for them, and re-layouts  4.07 us (4%)
    pallas_call x1, Pallas kernels, bin_rows(): pl.pallas_call(one_hot_kernel, grid=(rows // step_rows,), in_specs=[pl.Bl...  55.8 us
    pallas_call x1, Pallas kernels, spread(): pl.pallas_call(functools.partial(spread_kernel, n_lat, n_lon, side), out_...  47.9 us
    slice x1, local copies, waits for them, and re-layouts, body(): return overturn.reshape(BASINS, HIGH * LOW, -1)[:, :CLASSES]  4.07 us

profile of v2, /device:TPU:1, one launch (start us, length us, event | category | flops | bytes accessed | tf_op | source)
XLA Modules:
  0.0 107.8 jit_solution(8971314663757895769)
XLA Ops:
  0.0 55.8 %shard_map.46 = f32[28,2,16,128]{3,2,1,0:T(8,128)} custom-call(bf16[48,128,384]{2,1,0:T(8,128)(2,1)} %flow_ref.1, s32[48,128,384]{2,1,0:T(8,128)} %class_ref.1, s32[128,384]{1,0:T(8,128)} %basin_ref.1, s32[128,384]{1,0:T(8,128)} %depth_ref.1), custom_call_target="tpu_custom_call" | custom-call | tf_op jit(solution)/shard_map/pallas_call | solution.py:100
  55.8 47.9 %shard_map.47 = bf16[896,2048]{1,0:T(8,128)(2,1)} custom-call(f32[14,64,128]{2,1,0:T(8,128)} %bitcast.3), custom_call_target="tpu_custom_call" | custom-call | tf_op jit(solution)/shard_map/pallas_call | solution.py:261
  103.7 4.1 %slice.4 = bf16[4,200,2048]{2,1,0:T(8,128)(2,1)} slice(bf16[4,224,2048]{2,1,0:T(8,128)(2,1)} %bitcast.2), slice={[0:4], [0:200], [0:2048]} | slice | bytes 6553600 | tf_op jit(solution)/shard_map/slice | solution.py:284

commit v3 on v0

v3 whole, which is shorter than its diff:
```python
import functools

import jax
import jax.numpy as jnp
from jax import lax
from jax.experimental import pallas as pl
from jax.experimental.pallas import tpu as pltpu
from jax.sharding import PartitionSpec as P

CLASSES = 200
BASINS = 4
LOW = 32
HIGH = 7
SUB = 8
LANES = 128
SHARE = 4
PHASE = 4
SIDE = 4
MESH = pl.DeviceIdType.MESH


def overturn_kernel(
    n_lat, n_lon, flow_ref, class_ref, basin_ref, depth_ref, out_ref,
    table, parts, shuffle, lines, land,
    sum_send, sum_recv, z_send, z_recv, one_send, one_recv, two_send, two_recv, pair_send, pair_recv, out_sem,
):
    levels, rows, cols = class_ref.shape
    tiles = cols // LANES
    m = BASINS * HIGH * SUB
    n = LOW * SUB
    groups = LANES // SUB
    step = pl.program_id(0)
    steps = pl.num_programs(0)
    phases, owners, size, _ = table.shape
    chunk_rows = phases * size
    chunks = owners // 2
    depth = n_lon // 2
    lat, lon = lax.axis_index("lat"), lax.axis_index("lon")
    x, y = lat // SIDE, lax.rem(lat, SIDE)
    z, core = lon // 2, lax.rem(lon, 2)

    def at(to_lat, to_lon):
        return {"lat": to_lat, "lon": to_lon}

    def along(axis, d):
        if axis == 0:
            return lax.rem(x + d, SIDE) * SIDE + y
        return x * SIDE + lax.rem(y + d, SIDE)

    def block(chunk, of_lat):
        lines_of = pl.ds(pl.multiple_of((2 * chunk + core) * chunk_rows, chunk_rows), chunk_rows)
        return land.at[lines_of, pl.ds(pl.multiple_of(of_lat * LANES, LANES), LANES)]

    def send(src, dst, send_sem, recv_sem, to):
        return pltpu.make_async_remote_copy(
            src_ref=src, dst_ref=dst, send_sem=send_sem, recv_sem=recv_sem, device_id=to, device_id_type=MESH
        )

    barrier = pltpu.get_barrier_semaphore()

    @pl.when(step == 0)
    def _():
        for d in range(1, n_lon):
            pl.semaphore_signal(barrier, inc=1, device_id=at(lat, lax.rem(lon + d, n_lon)), device_id_type=MESH)
        for axis in range(2):
            for d in range(1, SIDE):
                pl.semaphore_signal(barrier, inc=1, device_id=at(along(axis, d), lon), device_id_type=MESH)
        line = lax.broadcasted_iota(jnp.int32, (LANES, LANES), 0)
        lane = lax.broadcasted_iota(jnp.int32, (LANES, LANES), 1) & (SUB - 1)
        for low in range(groups):
            at_low = pl.ds(low * LANES, LANES)
            shuffle[:LANES, at_low] = jnp.where(line == lane + low * SUB, 1.0, 0.0).astype(jnp.bfloat16)
            shuffle[LANES:, at_low] = jnp.zeros((LANES, LANES), jnp.bfloat16)
        pl.semaphore_wait(barrier, n_lon - 1 + 2 * (SIDE - 1))


    def twice(v):
        return jnp.concatenate([v, v - 1.0], axis=0).astype(jnp.bfloat16)

    digit = lax.broadcasted_iota(jnp.int32, (2 * LANES, LANES), 1) // (2 * SUB) * 2
    limits = [
        (digit + part * (LANES // SUB)).astype(jnp.float32).astype(jnp.bfloat16) for part in range(n // LANES)
    ]

    def add_products(sub, accs):
        r = pl.ds(sub * SUB, SUB)
        base = [basin_ref[r, pl.ds(tile * LANES, LANES)] * HIGH for tile in range(tiles)]
        wet_levels = [depth_ref[r, pl.ds(tile * LANES, LANES)] for tile in range(tiles)]
        halves = []
        for index in range(levels * tiles):
            k, tile = index // tiles, index % tiles
            c = pl.ds(tile * LANES, LANES)
            klass = class_ref[k, r, c]
            high = jnp.where(k < wet_levels[tile], base[tile] + (klass >> 5), -100)
            low = klass & (LOW - 1)
            flow = flow_ref[k, r, c].astype(jnp.float32)
            halves.append((
                twice(high.astype(jnp.float32)),
                twice(low.astype(jnp.float32)),
                jnp.concatenate([flow, flow], axis=0).astype(jnp.bfloat16),
            ))
            if len(halves) < 2:
                continue
            high2, low2, flow2 = [jnp.concatenate(h, axis=1) for h in zip(*halves)]
            halves = []
            zero = jnp.zeros_like(flow2)
            wide = jnp.concatenate([low2] * (LANES // (2 * SUB)), axis=0).T
            one = jnp.ones_like(wide)
            none = jnp.zeros_like(wide)
            rhs = jnp.concatenate([jnp.where(wide <= limit, one, none) for limit in limits], axis=1)
            lhs = jnp.concatenate(
                [jnp.where(high2 == jnp.bfloat16(2 * t), flow2, zero) for t in range(BASINS * HIGH // 2)], axis=0
            )
            q = (index // 2) % 2
            reg = (index // 4) % 2
            pltpu.matmul_push_rhs(rhs, staging_register=reg, mxu_index=q, transpose=False)
            pltpu.matmul_acc_lhs(accs[q], lhs, load_staged_rhs=reg)

    def finish(group, accs):
        row = lax.broadcasted_iota(jnp.int32, (1, SUB, n), 1)
        col = lax.broadcasted_iota(jnp.int32, (1, SUB, n), 2)
        own = (col & (SUB - 1)) == row
        lane = lax.broadcasted_iota(jnp.int32, (BASINS * HIGH, LANES), 1)
        both = pltpu.matmul_pop(accs[0]) + pltpu.matmul_pop(accs[1])
        part = jnp.sum(jnp.where(own, both.reshape(m // SUB, SUB, n), 0.0), axis=1)
        whole = jnp.where(lane >= LANES - SUB, part[:, n - LANES :], 0.0)
        for shift in (SUB, 2 * SUB, 4 * SUB, 8 * SUB):
            whole = whole + pltpu.roll(whole, shift, 1)
        for basin in range(BASINS):
            before = jnp.zeros((1, LANES), jnp.float32)
            for digit in range(HIGH):
                h = basin * HIGH + digit
                for half in range(n // LANES):
                    owner, share = (2 * h + half) // SHARE, (2 * h + half) % SHARE
                    table[group // PHASE, owner, pl.ds((group & (PHASE - 1)) * SHARE + share, 1), :] = (
                        part[h : h + 1, half * LANES : (half + 1) * LANES] + before
                    )
                before = before + whole[h : h + 1]


    def share_of(phase, d):
        to = lax.rem(lon + d, n_lon)
        return to, send(
            table.at[phase, lax.rem(to, owners)], parts.at[d - 1, phase],
            sum_send.at[phase, d - 1], sum_recv.at[phase, d - 1], at(lat, to),
        )

    def send_phase(phase):
        for d in range(1, n_lon):
            to, copy = share_of(phase, d)

            @pl.when(to < owners)
            def _():
                copy.start()

    def run(even, odd, moved):
        last = steps * 2
        add_products(0, even)
        finish((2 * step + last - 1) & (last - 1), odd)

        @pl.when((step > 0) & ((step & 1) == 0))
        def _():
            send_phase(step // 2 - 1)

        add_products(1, odd)
        finish(2 * step, even)

        @pl.when(step == steps - 1)
        def _():
            finish(last - 1, odd)
            send_phase(phases - 1)
            exchange(moved)


    def exchange(moved):
        partner = at(lat, z * 2 + 1 - core)

        def to_pair(chunk, of_lat):
            send(block(chunk, of_lat), block(chunk, of_lat), pair_send, pair_recv, partner).start()

        @pl.when(lon < owners)
        def _():
            totals = []
            for phase in range(phases):
                total = table[phase, lax.rem(lon, owners)]
                for d in range(1, n_lon):
                    share_of(phase, d)[1].wait_recv()
                    total = total + parts[d - 1, phase]
                totals.append(total)
            total = jnp.concatenate(totals, axis=0).astype(jnp.bfloat16)
            lhs = jnp.concatenate([total, jnp.zeros_like(total)], axis=1)
            row = lax.broadcasted_iota(jnp.int32, (chunk_rows, LANES), 0) // SHARE
            own = row == lax.broadcasted_iota(jnp.int32, (chunk_rows, LANES), 1) // SUB
            for piece in range(groups // 2):
                q = piece % 2
                pltpu.matmul_push_rhs(
                    shuffle[:, pl.ds(piece * 2 * LANES, 2 * LANES)], staging_register=0, mxu_index=q
                )
                pltpu.matmul_acc_lhs(moved[piece], lhs, load_staged_rhs=0)
            for piece in range(groups // 2):
                both = pltpu.matmul_pop(moved[piece])
                for half in range(2):
                    kept = jnp.where(own, both[:, half * LANES : (half + 1) * LANES], 0.0)
                    kept = jnp.sum(kept.reshape(chunk_rows // SUB, SUB, LANES), axis=0)
                    kept = kept[:SHARE] + kept[SHARE:]
                    for share in range(SHARE):
                        at_line = share * groups + piece * 2 + half
                        lines[at_line : at_line + 1, :] = kept[share : share + 1]
            block(z, lat)[...] = lines[...].astype(jnp.bfloat16)
            for d in range(1, depth):
                to = lax.rem(z + d, depth) * 2 + core
                send(block(z, lat), block(z, lat), z_send.at[d - 1], z_recv.at[z], at(lat, to)).start()

        def first(chunk, d):
            return send(block(chunk, lat), block(chunk, lat), one_send.at[chunk, d - 1], one_recv.at[chunk, d - 1],
                        at(along(chunk % 2, d), lon))

        def second(chunk, of, of_lat, d):
            return send(block(chunk, of_lat), block(chunk, of_lat), two_send, two_recv.at[chunk, of, d - 1],
                        at(along(1 - chunk % 2, d), lon))

        def came(chunk, d):
            return along(chunk % 2, SIDE - d)

        def came_twice(chunk, of, d):
            if chunk % 2 == 0:
                return lax.rem(x + (SIDE - of), SIDE) * SIDE + lax.rem(y + (SIDE - d), SIDE)
            return lax.rem(x + (SIDE - d), SIDE) * SIDE + lax.rem(y + (SIDE - of), SIDE)

        for chunk in range(chunks):

            @pl.when(z != chunk)
            def _():
                send(block(chunk, lat), block(chunk, lat), z_send.at[0], z_recv.at[chunk], at(lat, lon)).wait_recv()

            for d in range(1, SIDE):
                first(chunk, d).start()
            for d in range(1, SIDE):
                second(chunk, 0, lat, d).start()
            to_pair(chunk, lat)
        for chunk in range(chunks):
            for of in range(1, SIDE):
                first(chunk, of).wait_recv()
                for d in range(1, SIDE):
                    second(chunk, of, came(chunk, of), d).start()
                to_pair(chunk, came(chunk, of))
        for chunk in range(chunks):
            for of in range(SIDE):
                for d in range(1, SIDE):
                    second(chunk, of, lat, d).wait_recv()
                    to_pair(chunk, came_twice(chunk, of, d))

        half = land.at[pl.ds(0, chunks * chunk_rows)]
        pltpu.make_async_copy(half, half, pair_recv).wait()
        out = pltpu.make_async_copy(land, out_ref, out_sem)
        out.start()
        for phase in range(phases):
            for d in range(1, n_lon):
                to, copy = share_of(phase, d)

                @pl.when(to < owners)
                def _():
                    copy.wait_send()

        @pl.when(lon < owners)
        def _():
            for d in range(1, depth):
                send(block(z, lat), block(z, lat), z_send.at[d - 1], z_recv.at[z], at(lat, lon)).wait_send()

        for chunk in range(chunks):
            for d in range(1, SIDE):
                first(chunk, d).wait_send()
        seconds = land.at[pl.ds(0, chunks * SIDE * (SIDE - 1) * chunk_rows // n_lat)]
        pltpu.make_async_copy(seconds, seconds, two_send).wait()
        pltpu.make_async_copy(half, half, pair_send).wait()
        out.wait()

    def acc(q, lines_of):
        return pltpu.ACC(q)((lines_of, n), jnp.float32)

    pl.run_scoped(
        run,
        tuple(acc(q, m) for q in range(2)),
        tuple(acc(q, m) for q in range(2)),
        tuple(acc(piece % 2, chunk_rows) for piece in range(groups // 2)),
    )


def body(n_lat, n_lon, transport, sigma_class, basin_id, depth_levels):
    levels, rows, cols = sigma_class.shape
    step_rows = 2 * SUB
    owners = BASINS * HIGH * LOW * SUB // LANES // SHARE
    chunks = owners // 2
    phases = rows // SUB // PHASE
    size = SHARE * PHASE
    dma = pltpu.SemaphoreType.DMA
    everything = (owners * phases * size, n_lat * LANES)
    overturn = pl.pallas_call(
        functools.partial(overturn_kernel, n_lat, n_lon),
        grid=(rows // step_rows,),
        in_specs=[
            pl.BlockSpec((levels, step_rows, cols), lambda g: (0, g, 0)),
            pl.BlockSpec((levels, step_rows, cols), lambda g: (0, g, 0)),
            pl.BlockSpec((step_rows, cols), lambda g: (g, 0)),
            pl.BlockSpec((step_rows, cols), lambda g: (g, 0)),
        ],
        out_specs=pl.BlockSpec(memory_space=pl.ANY),
        out_shape=jax.ShapeDtypeStruct(everything, jnp.bfloat16),
        scratch_shapes=[
            pltpu.VMEM((phases, owners, size, LANES), jnp.float32),
            pltpu.VMEM((n_lon - 1, phases, size, LANES), jnp.float32),
            pltpu.VMEM((2 * LANES, LANES // SUB * LANES), jnp.bfloat16),
            pltpu.VMEM((phases * size, LANES), jnp.float32),
            pltpu.VMEM(everything, jnp.bfloat16),
            dma((phases, n_lon - 1)), dma((phases, n_lon - 1)),
            dma((n_lon // 2 - 1,)), dma((chunks,)),
            dma((chunks, SIDE - 1)), dma((chunks, SIDE - 1)),
            dma, dma((chunks, SIDE, SIDE - 1)),
            dma, dma, dma,
        ],
        compiler_params=pltpu.CompilerParams(
            collective_id=0, has_side_effects=True, dimension_semantics=("arbitrary",)
        ),
    )(transport, sigma_class, basin_id, depth_levels)
    return overturn.reshape(BASINS, HIGH * LOW, -1)[:, :CLASSES]


def solution(mesh):
    placed = (P(None, "lat", "lon"), P(None, "lat", "lon"), P("lat", "lon"), P("lat", "lon"))
    run = functools.partial(body, mesh.shape["lat"], mesh.shape["lon"])
    return jax.shard_map(run, mesh=mesh, in_specs=placed, out_specs=P(), check_vma=False)
```

time: 513 us -> 82.9 us (0.16)
  matrix products: 283 us -> 0 us
  waiting for transfers between devices: 106 us -> 0 us
  Pallas kernels: 0 us -> 78.7 us
  local copies, waits for them, and re-layouts: 51 us -> 4.07 us
  loops' own time: 33.8 us -> 0 us
  other arithmetic: 23 us -> 0 us
  between operations: 13.4 us -> 0.01 us
    dot_general x16 -> x0, matrix products: 283 us -> none  [one_block(): jnp.einsum('rcn,rbn->rbc', class_hot, basin_flow, preferred_element_type=...]
    all_gather x2 -> x0, waiting for transfers between devices: 106 us -> none  [the longest x1 54.4 us: body(): return lax.all_gather(overturn, 'lat', axis=2, tiled=True)]
    pallas_call x0 -> x1, Pallas kernels: none -> 78.7 us  [body(): pl.pallas_call(functools.partial(overturn_kernel, n_lat, n_lon), grid=(ro...]
    dynamic_slice x48 -> x0, local copies, waits for them, and re-layouts: 44.4 us -> none  [the longest x16 21.4 us: one_block(): lax.dynamic_slice_in_dim(sigma_class, start, block_rows, 1)]
    another operation x1 -> x0, loops' own time: 33.8 us -> none  [bin_rows(): tables = lax.map(one_block, starts)]
    select_n x16 -> x0, other arithmetic: 19.1 us -> none  [one_block(): jnp.where(wet_cells, flow, jnp.zeros_like(flow))]
  transfers between devices with their start and end apart: 2 -> 0, of which waited for: 2 -> 0; matrix products, arithmetic and copies ran while one was open for 0% -> 0% of each run, Pallas kernels for 0% -> 0%
where the time goes in v3:
time: 82.9 us; the launch traced here: 82.8 us
  Pallas kernels  78.7 us (95%)
  local copies, waits for them, and re-layouts  4.07 us (5%)
    pallas_call x1, Pallas kernels, body(): pl.pallas_call(functools.partial(overturn_kernel, n_lat, n_lon), grid=(ro...  78.7 us
    slice x1, local copies, waits for them, and re-layouts, body(): return overturn.reshape(BASINS, HIGH * LOW, -1)[:, :CLASSES]  4.07 us

profile of v3, /device:TPU:1, one launch (start us, length us, event | category | flops | bytes accessed | tf_op | source)
XLA Modules:
  0.0 82.8 jit_solution(6742430458101179683)
XLA Ops:
  0.0 78.7 %shard_map.46 = bf16[896,2048]{1,0:T(8,128)(2,1)} custom-call(bf16[48,128,384]{2,1,0:T(8,128)(2,1)} %flow_ref.1, s32[48,128,384]{2,1,0:T(8,128)} %class_ref.1, s32[128,384]{1,0:T(8,128)} %basin_ref.1, s32[128,384]{1,0:T(8,128)} %depth_ref.1), custom_call_target="tpu_custom_call" | custom-call | tf_op jit(solution)/shard_map/pallas_call | solution.py:298
  78.7 4.1 %slice.4 = bf16[4,200,2048]{2,1,0:T(8,128)(2,1)} slice(bf16[4,224,2048]{2,1,0:T(8,128)(2,1)} %bitcast.1), slice={[0:4], [0:200], [0:2048]} | slice | bytes 6553600 | tf_op jit(solution)/shard_map/slice | solution.py:325

commit v4 on v3

--- a/solution.py
+++ b/solution.py
@@ -49,7 +49,7 @@
 
     def block(chunk, of_lat):
         lines_of = pl.ds(pl.multiple_of((2 * chunk + core) * chunk_rows, chunk_rows), chunk_rows)
-        return land.at[lines_of, pl.ds(pl.multiple_of(of_lat * LANES, LANES), LANES)]
+        return land.at[of_lat, lines_of]
 
     def send(src, dst, send_sem, recv_sem, to):
         return pltpu.make_async_remote_copy(
@@ -211,49 +211,60 @@
                 to = lax.rem(z + d, depth) * 2 + core
                 send(block(z, lat), block(z, lat), z_send.at[d - 1], z_recv.at[z], at(lat, to)).start()
 
+        def across(chunk, d_one, d_two):
+            swap = lax.rem(chunk, 2)
+            dx = d_one + swap * (d_two - d_one)
+            dy = d_two + swap * (d_one - d_two)
+            return lax.rem(x + dx, SIDE) * SIDE + lax.rem(y + dy, SIDE)
+
         def first(chunk, d):
             return send(block(chunk, lat), block(chunk, lat), one_send.at[chunk, d - 1], one_recv.at[chunk, d - 1],
-                        at(along(chunk % 2, d), lon))
+                        at(across(chunk, d, 0), lon))
 
         def second(chunk, of, of_lat, d):
             return send(block(chunk, of_lat), block(chunk, of_lat), two_send, two_recv.at[chunk, of, d - 1],
-                        at(along(1 - chunk % 2, d), lon))
-
-        def came(chunk, d):
-            return along(chunk % 2, SIDE - d)
-
-        def came_twice(chunk, of, d):
-            if chunk % 2 == 0:
-                return lax.rem(x + (SIDE - of), SIDE) * SIDE + lax.rem(y + (SIDE - d), SIDE)
-            return lax.rem(x + (SIDE - d), SIDE) * SIDE + lax.rem(y + (SIDE - of), SIDE)
-
-        for chunk in range(chunks):
-
-            @pl.when(z != chunk)
-            def _():
+                        at(across(chunk, 0, d), lon))
+
+        def nearest_first(visit):
+            for hop in sorted(range(depth), key=lambda hop: min(hop, depth - hop)):
+                chunk = lax.rem(z + hop, depth)
+                pl.when(chunk < chunks)(functools.partial(visit, chunk, hop))
+
+        def arrive(chunk, hop):
+            if hop:
                 send(block(chunk, lat), block(chunk, lat), z_send.at[0], z_recv.at[chunk], at(lat, lon)).wait_recv()
-
             for d in range(1, SIDE):
                 first(chunk, d).start()
             for d in range(1, SIDE):
                 second(chunk, 0, lat, d).start()
             to_pair(chunk, lat)
-        for chunk in range(chunks):
+
+        def turn(chunk, hop):
             for of in range(1, SIDE):
                 first(chunk, of).wait_recv()
+                came = across(chunk, SIDE - of, 0)
                 for d in range(1, SIDE):
-                    second(chunk, of, came(chunk, of), d).start()
-                to_pair(chunk, came(chunk, of))
-        for chunk in range(chunks):
+                    second(chunk, of, came, d).start()
+                to_pair(chunk, came)
+
+        def settle(chunk, hop):
             for of in range(SIDE):
                 for d in range(1, SIDE):
                     second(chunk, of, lat, d).wait_recv()
-                    to_pair(chunk, came_twice(chunk, of, d))
-
-        half = land.at[pl.ds(0, chunks * chunk_rows)]
+                    to_pair(chunk, across(chunk, SIDE - of, SIDE - d))
+
+        nearest_first(arrive)
+        nearest_first(turn)
+        nearest_first(settle)
+
+        half = land.at[pl.ds(0, n_lat // 2)]
         pltpu.make_async_copy(half, half, pair_recv).wait()
-        out = pltpu.make_async_copy(land, out_ref, out_sem)
-        out.start()
+        outs = [
+            pltpu.make_async_copy(land.at[of], out_ref.at[:, pl.ds(of * LANES, LANES)], out_sem.at[of])
+            for of in range(n_lat)
+        ]
+        for out in outs:
+            out.start()
         for phase in range(phases):
             for d in range(1, n_lon):
                 to, copy = share_of(phase, d)
@@ -270,10 +281,11 @@
         for chunk in range(chunks):
             for d in range(1, SIDE):
                 first(chunk, d).wait_send()
-        seconds = land.at[pl.ds(0, chunks * SIDE * (SIDE - 1) * chunk_rows // n_lat)]
+        seconds = land.at[pl.ds(0, chunks * SIDE * (SIDE - 1) * chunk_rows // land.shape[1])]
         pltpu.make_async_copy(seconds, seconds, two_send).wait()
         pltpu.make_async_copy(half, half, pair_send).wait()
-        out.wait()
+        for out in outs:
+            out.wait()
 
     def acc(q, lines_of):
         return pltpu.ACC(q)((lines_of, n), jnp.float32)
@@ -284,6 +296,20 @@
         tuple(acc(q, m) for q in range(2)),
         tuple(acc(piece % 2, chunk_rows) for piece in range(groups // 2)),
     )
+
+
+def keep_kernel(all_ref, kept_ref, held, in_sem, out_sem):
+    ins = [
+        pltpu.make_async_copy(all_ref.at[b, pl.ds(0, CLASSES)], held.at[b], in_sem.at[b]) for b in range(BASINS)
+    ]
+    outs = [pltpu.make_async_copy(held.at[b], kept_ref.at[b], out_sem.at[b]) for b in range(BASINS)]
+    for copy in ins:
+        copy.start()
+    for b in range(BASINS):
+        ins[b].wait()
+        outs[b].start()
+    for copy in outs:
+        copy.wait()
 
 
 def body(n_lat, n_lon, transport, sigma_class, basin_id, depth_levels):
@@ -311,18 +337,25 @@
             pltpu.VMEM((n_lon - 1, phases, size, LANES), jnp.float32),
             pltpu.VMEM((2 * LANES, LANES // SUB * LANES), jnp.bfloat16),
             pltpu.VMEM((phases * size, LANES), jnp.float32),
-            pltpu.VMEM(everything, jnp.bfloat16),
+            pltpu.VMEM((n_lat, everything[0], LANES), jnp.bfloat16),
             dma((phases, n_lon - 1)), dma((phases, n_lon - 1)),
             dma((n_lon // 2 - 1,)), dma((chunks,)),
             dma((chunks, SIDE - 1)), dma((chunks, SIDE - 1)),
             dma, dma((chunks, SIDE, SIDE - 1)),
-            dma, dma, dma,
+            dma, dma, dma((n_lat,)),
         ],
         compiler_params=pltpu.CompilerParams(
             collective_id=0, has_side_effects=True, dimension_semantics=("arbitrary",)
         ),
     )(transport, sigma_class, basin_id, depth_levels)
-    return overturn.reshape(BASINS, HIGH * LOW, -1)[:, :CLASSES]
+    kept = jax.ShapeDtypeStruct((BASINS, CLASSES, n_lat * LANES), jnp.bfloat16)
+    return pl.pallas_call(
+        keep_kernel,
+        out_shape=kept,
+        in_specs=[pl.BlockSpec(memory_space=pl.ANY)],
+        out_specs=pl.BlockSpec(memory_space=pl.ANY),
+        scratch_shapes=[pltpu.VMEM(kept.shape, kept.dtype), dma((BASINS,)), dma((BASINS,))],
+    )(overturn.reshape(BASINS, HIGH * LOW, -1))
 
 
 def solution(mesh):

time: 82.9 us -> 81.9 us (0.988)
  local copies, waits for them, and re-layouts: 4.07 us -> 0 us
  Pallas kernels: 78.7 us -> 81.8 us
    slice x1 -> x0, local copies, waits for them, and re-layouts: 4.07 us -> none  [body(): return overturn.reshape(BASINS, HIGH * LOW, -1)[:, :CLASSES]]
    pallas_call x0 -> x1, Pallas kernels: none -> 2.91 us  [body(): pl.pallas_call(keep_kernel, out_shape=kept, in_specs=[pl.BlockSpec(memory...]
where the time goes in v4:
time: 81.9 us; the launch traced here: 81.8 us
  Pallas kernels  81.8 us (100%)
    pallas_call x1, Pallas kernels, body(): pl.pallas_call(functools.partial(overturn_kernel, n_lat, n_lon), grid=(ro...  78.8 us
    pallas_call x1, Pallas kernels, body(): pl.pallas_call(keep_kernel, out_shape=kept, in_specs=[pl.BlockSpec(memory...  2.91 us

profile of v4, /device:TPU:1, one launch (start us, length us, event | category | flops | bytes accessed | tf_op | source)
XLA Modules:
  0.0 81.8 jit_solution(10845657599429291822)
XLA Ops:
  0.0 78.8 %shard_map.46 = bf16[896,2048]{1,0:T(8,128)(2,1)} custom-call(bf16[48,128,384]{2,1,0:T(8,128)(2,1)} %flow_ref.1, s32[48,128,384]{2,1,0:T(8,128)} %class_ref.1, s32[128,384]{1,0:T(8,128)} %basin_ref.1, s32[128,384]{1,0:T(8,128)} %depth_ref.1), custom_call_target="tpu_custom_call" | custom-call | tf_op jit(solution)/shard_map/pallas_call | solution.py:324
  78.9 2.9 %shard_map.47 = bf16[4,200,2048]{2,1,0:T(8,128)(2,1)} custom-call(bf16[4,224,2048]{2,1,0:T(8,128)(2,1)} %bitcast.1), custom_call_target="tpu_custom_call" | custom-call | tf_op jit(solution)/shard_map/pallas_call | solution.py:352

commit v5 on v4

--- a/solution.py
+++ b/solution.py
@@ -14,7 +14,7 @@
 SUB = 8
 LANES = 128
 SHARE = 4
-PHASE = 4
+PHASE = 2
 SIDE = 4
 MESH = pl.DeviceIdType.MESH
 
@@ -71,7 +71,6 @@
             at_low = pl.ds(low * LANES, LANES)
             shuffle[:LANES, at_low] = jnp.where(line == lane + low * SUB, 1.0, 0.0).astype(jnp.bfloat16)
             shuffle[LANES:, at_low] = jnp.zeros((LANES, LANES), jnp.bfloat16)
-        pl.semaphore_wait(barrier, n_lon - 1 + 2 * (SIDE - 1))
 
 
     def twice(v):
@@ -158,9 +157,18 @@
         add_products(0, even)
         finish((2 * step + last - 1) & (last - 1), odd)
 
+        @pl.when(step == 2)
+        def _():
+            pl.semaphore_wait(barrier, n_lon - 1 + 2 * (SIDE - 1))
+
         @pl.when((step > 0) & ((step & 1) == 0))
         def _():
-            send_phase(step // 2 - 1)
+            send_phase(step - 2)
+            send_phase(step - 1)
+
+        @pl.when(step == steps - 1)
+        def _():
+            send_phase(phases - 2)
 
         add_products(1, odd)
         finish(2 * step, even)
@@ -212,7 +220,7 @@
                 send(block(z, lat), block(z, lat), z_send.at[d - 1], z_recv.at[z], at(lat, to)).start()
 
         def across(chunk, d_one, d_two):
-            swap = lax.rem(chunk, 2)
+            swap = lax.rem(chunk + core, 2)
             dx = d_one + swap * (d_two - d_one)
             dy = d_two + swap * (d_one - d_two)
             return lax.rem(x + dx, SIDE) * SIDE + lax.rem(y + dy, SIDE)

time: 81.9 us -> 78.3 us (0.956)
  Pallas kernels: 81.8 us -> 78.2 us
    pallas_call x1, Pallas kernels: 78.8 us -> 75.3 us  [body(): pl.pallas_call(functools.partial(overturn_kernel, n_lat, n_lon), grid=(ro...]
where the time goes in v5:
time: 78.3 us; the launch traced here: 78.2 us
  Pallas kernels  78.2 us (100%)
    pallas_call x1, Pallas kernels, body(): pl.pallas_call(functools.partial(overturn_kernel, n_lat, n_lon), grid=(ro...  75.3 us
    pallas_call x1, Pallas kernels, body(): pl.pallas_call(keep_kernel, out_shape=kept, in_specs=[pl.BlockSpec(memory...  2.91 us

profile of v5, /device:TPU:1, one launch (start us, length us, event | category | flops | bytes accessed | tf_op | source)
XLA Modules:
  0.0 78.2 jit_solution(15114801004638975916)
XLA Ops:
  0.0 75.3 %shard_map.46 = bf16[896,2048]{1,0:T(8,128)(2,1)} custom-call(bf16[48,128,384]{2,1,0:T(8,128)(2,1)} %flow_ref.1, s32[48,128,384]{2,1,0:T(8,128)} %class_ref.1, s32[128,384]{1,0:T(8,128)} %basin_ref.1, s32[128,384]{1,0:T(8,128)} %depth_ref.1), custom_call_target="tpu_custom_call" | custom-call | tf_op jit(solution)/shard_map/pallas_call | solution.py:332
  75.3 2.9 %shard_map.47 = bf16[4,200,2048]{2,1,0:T(8,128)(2,1)} custom-call(bf16[4,224,2048]{2,1,0:T(8,128)(2,1)} %bitcast.1), custom_call_target="tpu_custom_call" | custom-call | tf_op jit(solution)/shard_map/pallas_call | solution.py:360

commit v6 on v5

--- a/solution.py
+++ b/solution.py
@@ -183,6 +183,17 @@
     def exchange(moved):
         partner = at(lat, z * 2 + 1 - core)
 
+        def shares_left(phase):
+            for d in range(1, n_lon):
+                to, copy = share_of(phase, d)
+
+                @pl.when(to < owners)
+                def _():
+                    copy.wait_send()
+
+        for phase in range(phases - 1):
+            shares_left(phase)
+
         def to_pair(chunk, of_lat):
             send(block(chunk, of_lat), block(chunk, of_lat), pair_send, pair_recv, partner).start()
 
@@ -215,7 +226,7 @@
                         at_line = share * groups + piece * 2 + half
                         lines[at_line : at_line + 1, :] = kept[share : share + 1]
             block(z, lat)[...] = lines[...].astype(jnp.bfloat16)
-            for d in range(1, depth):
+            for d in sorted(range(1, depth), key=lambda d: min(d, depth - d)):
                 to = lax.rem(z + d, depth) * 2 + core
                 send(block(z, lat), block(z, lat), z_send.at[d - 1], z_recv.at[z], at(lat, to)).start()
 
@@ -261,8 +272,18 @@
                     second(chunk, of, lat, d).wait_recv()
                     to_pair(chunk, across(chunk, SIDE - of, SIDE - d))
 
+        shares_left(phases - 1)
         nearest_first(arrive)
         nearest_first(turn)
+
+        @pl.when(lon < owners)
+        def _():
+            for d in range(1, depth):
+                send(block(z, lat), block(z, lat), z_send.at[d - 1], z_recv.at[z], at(lat, lon)).wait_send()
+
+        for chunk in range(chunks):
+            for d in range(1, SIDE):
+                first(chunk, d).wait_send()
         nearest_first(settle)
 
         half = land.at[pl.ds(0, n_lat // 2)]
@@ -273,22 +294,6 @@
         ]
         for out in outs:
             out.start()
-        for phase in range(phases):
-            for d in range(1, n_lon):
-                to, copy = share_of(phase, d)
-
-                @pl.when(to < owners)
-                def _():
-                    copy.wait_send()
-
-        @pl.when(lon < owners)
-        def _():
-            for d in range(1, depth):
-                send(block(z, lat), block(z, lat), z_send.at[d - 1], z_recv.at[z], at(lat, lon)).wait_send()
-
-        for chunk in range(chunks):
-            for d in range(1, SIDE):
-                first(chunk, d).wait_send()
         seconds = land.at[pl.ds(0, chunks * SIDE * (SIDE - 1) * chunk_rows // land.shape[1])]
         pltpu.make_async_copy(seconds, seconds, two_send).wait()
         pltpu.make_async_copy(half, half, pair_send).wait()

time: 78.3 us -> 77.6 us (level)
  no operation moved by 1% of the time
where the time goes in v6:
time: 77.6 us; the launch traced here: 77.5 us
  Pallas kernels  77.5 us (100%)
    pallas_call x1, Pallas kernels, body(): pl.pallas_call(functools.partial(overturn_kernel, n_lat, n_lon), grid=(ro...  74.6 us
    pallas_call x1, Pallas kernels, body(): pl.pallas_call(keep_kernel, out_shape=kept, in_specs=[pl.BlockSpec(memory...  2.91 us

profile of v6, /device:TPU:1, one launch (start us, length us, event | category | flops | bytes accessed | tf_op | source)
XLA Modules:
  0.0 77.5 jit_solution(7112982888786974523)
XLA Ops:
  0.0 74.6 %shard_map.46 = bf16[896,2048]{1,0:T(8,128)(2,1)} custom-call(bf16[48,128,384]{2,1,0:T(8,128)(2,1)} %flow_ref.1, s32[48,128,384]{2,1,0:T(8,128)} %class_ref.1, s32[128,384]{1,0:T(8,128)} %basin_ref.1, s32[128,384]{1,0:T(8,128)} %depth_ref.1), custom_call_target="tpu_custom_call" | custom-call | tf_op jit(solution)/shard_map/pallas_call | solution.py:337
  74.6 2.9 %shard_map.47 = bf16[4,200,2048]{2,1,0:T(8,128)(2,1)} custom-call(bf16[4,224,2048]{2,1,0:T(8,128)(2,1)} %bitcast.1), custom_call_target="tpu_custom_call" | custom-call | tf_op jit(solution)/shard_map/pallas_call | solution.py:365
